TPU v7x, 32 devices: a whole 2x2x4 slice. The times are simulated.
32 devices in a mesh: parts: 2 (over x), genes: 8 (over z, y), samples: 2 (over core).
Axes of the slice: x: 2, y: 2, z: 4, core: 2. Of those that a mesh axis runs over, the one named last changes fastest.
Arguments:
- dosage: bfloat16 [32768, 2048], P(('parts', 'genes'), 'samples'), parts along dimension 0, may hold values from -6 to 6
- expression: bfloat16 [128, 2048], P(('parts', 'genes'), 'samples'), parts along dimension 0, may hold values from -6 to 6
- intron_counts: bfloat16 [4096, 2560], P(('parts', 'samples', 'genes')), parts along dimension 0, may hold values from 1 to 100
- cluster_sizes: int32 [128, 8], P('parts'), parts along dimension 0, may hold values from 1 to 12, 40 in all within a row
- valid_mask: int32 [128, 40], P('parts'), parts along dimension 0, may hold values 0 or 1
- gene_block: int32 [128], P('parts'), parts along dimension 0, may hold values from 0 to 63, each once
- window_start: int32 [128], P(('parts', 'genes')), parts along dimension 0, may hold values from 0 to 1024, as said below
Outputs:
- assoc: bfloat16 [128, 41, 2048], P(('parts', 'genes'), None, 'samples'), parts along dimension 0
There are 2 independent parts, one for each index of `parts`. A program takes and returns all parts, laid end to end along the dimension named above; each array names one. Nothing has to cross between parts.
Inputs may be any that keep to these rules, and one draw needn't show every extreme that they name: Every window_start is a multiple of 128 and at most 1024; some gene reaches 1024 in every draw. `gene_block`: a permutation of the genes. `cluster_sizes`: each row sums to 40.
All inputs are finite; a program needn't handle non-finite values.
Results may differ from a plain program's by a relative error of at most 0.0058.
Values may be sent and summed in bfloat16 or wider, within the bound.
A program may use at most 64 MiB of HBM per device.

v0:
```python
import jax
import jax.numpy as jnp
from jax import lax
from jax.sharding import PartitionSpec as P

W = 2048
SLOTS = 40
SPILL = 1024
ALIGN = 128


def shifted(block, axis, distance):
    devices = range(lax.axis_size(axis))
    route = [(i - distance, i) for i in devices if i - distance in devices]
    return lax.ppermute(block, axis, route)


def cluster_ratios(counts, cluster_sizes, valid_mask):
    cluster_ends = jnp.cumsum(cluster_sizes, axis=1, dtype=jnp.int32)
    slot_index = jnp.arange(SLOTS, dtype=jnp.int32)
    cluster_id = jnp.sum(
        (cluster_ends[:, None, :] <= slot_index[None, :, None]).astype(jnp.int32),
        axis=2,
        dtype=jnp.int32,
    )
    same_cluster = (cluster_id[:, :, None] == cluster_id[:, None, :]).astype(jnp.float32)
    live_counts = counts * valid_mask.astype(jnp.float32)[None, :, :]
    cluster_total = jnp.einsum(
        "sgj,gjk->sgk", live_counts, same_cluster, precision=lax.Precision.HIGHEST
    )
    return (live_counts / jnp.maximum(cluster_total, 1.0)).astype(jnp.bfloat16)


def tile_window(owner_block, offset, width):
    leading = owner_block.shape[:-1]
    tiles = owner_block.reshape(leading + (owner_block.shape[-1] // ALIGN, ALIGN))
    first_tile = offset // ALIGN
    piece = lax.dynamic_slice_in_dim(tiles, first_tile, width // ALIGN, len(leading))
    return piece.reshape(leading + (width,))


def window_slices(product, row_sum, row_square, starts, width):

    def window_of(owner_block, offset):
        return tile_window(owner_block, offset, width)

    cross_part = jax.vmap(window_of, in_axes=(0, 0))(product, starts)
    sum_part = jax.vmap(window_of, in_axes=(None, 0))(row_sum, starts)
    square_part = jax.vmap(window_of, in_axes=(None, 0))(row_square, starts)
    return (cross_part, sum_part, square_part)


def finish_stats(cross_part, sum_part, square_part, phen_sum, phen_square, sample_count):
    numerator = cross_part - sum_part[:, None, :] * phen_sum[:, :, None] / sample_count
    dose_var = jnp.maximum(square_part - sum_part * sum_part / sample_count, 1.0)
    pheno_var = jnp.maximum(phen_square - phen_sum * phen_sum / sample_count, 1.0)
    return (numerator * lax.rsqrt(dose_var)[:, None, :] * lax.rsqrt(pheno_var)[:, :, None]).astype(
        jnp.bfloat16
    )


def shards(dosage, expression, intron_counts, cluster_sizes, valid_mask, gene_block, window_start):
    samp_dev = dosage.shape[1]
    gene_dev = expression.shape[0]
    total_genes = gene_block.shape[0]
    next_rows = shifted(dosage[:SPILL], "genes", -1)
    dose_rows = jnp.concatenate([dosage, next_rows], axis=0)
    stored = intron_counts.reshape(intron_counts.shape[0], total_genes, SLOTS)
    counts = jnp.take(stored, gene_block, axis=1).astype(jnp.float32)
    ratios = cluster_ratios(counts, cluster_sizes, valid_mask).reshape(
        intron_counts.shape[0], total_genes * SLOTS
    )
    exchanged = lax.all_to_all(ratios, "genes", split_axis=1, concat_axis=0, tiled=True)
    intron_panel = exchanged.reshape(samp_dev, gene_dev, SLOTS)
    n_samples = lax.axis_size("samples")
    half_width = W // n_samples
    offset = lax.axis_index("samples") * half_width
    contract = (((0,), (1,)), ((), ()))
    expr_product = lax.dot_general(
        expression, dose_rows, (((1,), (1,)), ((), ())), preferred_element_type=jnp.float32
    )
    intron_product = lax.dot_general(
        exchanged, dose_rows, contract, preferred_element_type=jnp.float32
    )
    intron_product = intron_product.reshape(gene_dev, SLOTS, W + SPILL)
    product = jnp.concatenate([expr_product[:, None, :], intron_product], axis=1)
    expr_float = expression.astype(jnp.float32)
    intron_float = intron_panel.astype(jnp.float32)
    phen_sum = jnp.concatenate(
        [jnp.sum(expr_float, axis=1)[:, None], jnp.sum(intron_float, axis=0)], axis=1
    )
    phen_square = jnp.concatenate(
        [
            jnp.sum(expr_float * expr_float, axis=1)[:, None],
            jnp.sum(intron_float * intron_float, axis=0),
        ],
        axis=1,
    )
    dose_float = dose_rows.astype(jnp.float32)
    row_sum = jnp.sum(dose_float, axis=1)
    row_square = jnp.sum(dose_float * dose_float, axis=1)
    row_sum, row_square, phen_sum, phen_square = lax.psum(
        (row_sum, row_square, phen_sum, phen_square), "samples"
    )
    cross_part, sum_part, square_part = window_slices(product, row_sum, row_square, window_start, W)
    cross_sums = lax.psum_scatter(cross_part, "samples", scatter_dimension=2, tiled=True)
    sum_half = lax.dynamic_slice_in_dim(sum_part, offset, half_width, 1)
    square_half = lax.dynamic_slice_in_dim(square_part, offset, half_width, 1)
    sample_count = float(samp_dev * n_samples)
    return finish_stats(cross_sums, sum_half, square_half, phen_sum, phen_square, sample_count)


def solution(mesh):
    in_specs = (
        P(("parts", "genes"), "samples"),
        P(("parts", "genes"), "samples"),
        P(("parts", "samples", "genes"), None),
        P("parts", None),
        P("parts", None),
        P("parts"),
        P(("parts", "genes")),
    )
    out_specs = P(("parts", "genes"), None, "samples")
    return jax.shard_map(shards, mesh=mesh, in_specs=in_specs, out_specs=out_specs, check_vma=False)
```

profile of v0, /device:TPU:0, one launch (start us, length us, event | category | flops | bytes accessed | tf_op | source)
XLA Modules:
  0.0 140.2 jit_solution(9824551427102057853)
XLA Ops:
  6.5 3.2 %slice.3 = bf16[1024,1024]{1,0:T(8,128)(2,1)} slice(bf16[2048,1024]{1,0:T(8,128)(2,1)} %param.7), slice={[0:1024], [0:1024]} | slice | bytes 4194304 | tf_op jit(solution)/shard_map/slice | solution.py:66
  9.7 1.3 collective-permute-start
  11.7 0.7 gather_fusion
  12.4 3.1 %fusion.3 = bf16[128,64,40]{0,2,1:T(8,128)(2,1)} fusion(f32[64,40]{1,0:T(8,128)S(1)} %copy.35, bf16[64,128,40]{1,2,0:T(8,128)(2,1)S(1)} %gather_fusion, s32[64,40]{1,0:T(8,128)S(1)} %copy.36, pred[64]{0:T(512)(128)(4,1)S(1)} %compare_and_fusion), kind=kOutput, calls=%fused_computation.15 | convolution fusion | flops 160337920 | bytes 1331264 | tf_op jit(solution)/shard_map/sgj,gjk->sgk/dot_general | solution.py:28
  15.5 8.6 %all-to-all-start = ((bf16[128,8,320]{0,2,1:T(8,128)(2,1)}), bf16[128,8,320]{0,2,1:T(8,128)(2,1)S(1)}, u32[]{:S(2)}, u32[]{:S(2)}) async-start(bf16[128,8,320]{0,2,1:T(8,128)(2,1)} %bitcast.5), calls=%async_computation | async-start | bytes 1310720 | tf_op jit(solution)/shard_map/all_to_all | solution.py:73
  24.1 4.6 %constant_dynamic-update-slice_fusion.1 = bf16[3072,1024]{1,0:T(8,128)(2,1)} fusion(bf16[2048,1024]{1,0:T(8,128)(2,1)} %param.7), kind=kLoop, calls=%fused_computation.40 | loop fusion | bytes 8388608
  28.7 49.8 %all-to-all-done = bf16[128,8,320]{0,2,1:T(8,128)(2,1)S(1)} async-done(((bf16[128,8,320]{0,2,1:T(8,128)(2,1)}), bf16[128,8,320]{0,2,1:T(8,128)(2,1)S(1)}, u32[]{:S(2)}, u32[]{:S(2)}) %all-to-all-start) | async-done | bytes 655392 | tf_op jit(solution)/shard_map/all_to_all | solution.py:73
  78.6 1.5 %constant_dynamic-update-slice_fusion = bf16[3072,1024]{1,0:T(8,128)(2,1)} fusion(bf16[3072,1024]{1,0:T(8,128)(2,1)} %constant_dynamic-update-slice_fusion.1, bf16[1024,1024]{1,0:T(8,128)(2,1)S(1)} %collective-permute-done), kind=kLoop, calls=%fused_computation.39 | loop fusion | bytes 4194304 | tf_op jit(solution)/shard_map/concatenate | solution.py:67
  80.1 4.7 %convolution_bitcast_fusion = f32[8,1,24,128]{3,0,2,1:T(8,128)S(1)} fusion(bf16[3072,1024]{1,0:T(8,128)(2,1)} %constant_dynamic-update-slice_fusion, bf16[8,1024]{1,0:T(8,128)(2,1)S(1)} %copy-done.4), kind=kOutput, calls=%fused_computation.22 | convolution fusion | flops 50331648 | bytes 6406144 | tf_op jit(solution)/shard_map/dot_general | solution.py:79
  84.9 2.3 %fusion.18 = f32[8,40,24,128]{3,1,2,0:T(8,128)S(1)} fusion(bf16[8,40,1024,1]{2,1,3,0:T(8,128)(2,1)S(1)} %bitcast.75, bf16[24,128,1024,1]{2,1,0,3:T(8,128)(2,1)S(1)} %bitcast.73), kind=kOutput, calls=%fused_computation.55 | convolution fusion | flops 2013265920 | bytes 10878976 | tf_op jit(solution)/shard_map/dot_general | solution.py:82
  87.2 0.5 pad_maximum_fusion
  87.7 2.7 %copy.40 = f32[8,41,24,128]{3,1,0,2:T(8,128)} copy(f32[8,41,24,128]{3,1,2,0:T(8,128)S(1)} %pad_maximum_fusion) | data formatting | bytes 8060928 | tf_op jit(solution)/shard_map/concatenate | solution.py:86
  90.4 3.1 %gather_fusion.1 = f32[8,41,16,128]{3,1,2,0:T(8,128)S(1)} fusion(f32[8,41,24,128]{3,1,0,2:T(8,128)} %copy.40, s32[8]{0:T(128)S(1)} %or_bitcast_fusion), kind=kCustom, calls=%fused_computation.1 | custom fusion | bytes 5374080 | tf_op jit(solution)/shard_map/vmap()/gather | solution.py:38
  93.5 2.4 %copy.41 = f32[8,41,16,128]{3,2,0,1:T(8,128)} copy(f32[8,41,16,128]{3,1,2,0:T(8,128)S(1)} %gather_fusion.1) | data formatting | bytes 5373952 | tf_op jit(solution)/shard_map/vmap()/gather | solution.py:38
  95.9 3.9 %reshape.50 = f32[8,41,2048]{2,0,1:T(8,128)} reshape(f32[8,41,16,128]{3,2,0,1:T(8,128)} %copy.41) | data formatting | bytes 5373952 | tf_op jit(solution)/shard_map/vmap()/reshape | solution.py:39
  100.2 0.7 copy-done.2
  101.4 5.5 %convert_reduce_fusion = (f32[3072]{0:T(1024)S(1)}, f32[3072]{0:T(1024)S(1)}) fusion(bf16[3072,1024]{1,0:T(8,128)(2,1)} %constant_dynamic-update-slice_fusion), kind=kLoop, calls=%fused_computation.7 | loop fusion | flops 12576768 | bytes 6316032 | tf_op jit(solution)/shard_map/reduce_sum | solution.py:100
  106.9 3.4 %all-reduce.1 = (f32[8,41]{1,0:T(8,128)S(1)}, f32[8,41]{1,0:T(8,128)S(1)}, f32[24,128]{1,0:T(8,128)S(1)}, f32[24,128]{1,0:T(8,128)S(1)}) all-reduce(f32[8,41]{1,0:T(8,128)S(1)} %get-tuple-element.50, f32[8,41]{1,0:T(8,128)S(1)} %get-tuple-element.49, ...), channel_id=1, replica_groups=mesh['parts'=2,'genes'=8,'samples'=2] {'samples'}, use_global_device_ids=true, to_apply=%region_12.13 | all-reduce | flops 6800 | bytes 54400 | tf_op jit(solution)/shard_map/psum | solution.py:102
  110.3 10.1 %while.3 = (s32[]{:T(128)}, f32[24,128]{1,0:T(8,128)S(1)}, s32[8,2]{0,1:T(2,128)S(1)}, f32[8,16,128]{2,1,0:T(8,128)S(1)}, s32[]{:T(128)}) while((s32[]{:T(128)}, f32[24,128]{1,0:T(8,128)S(1)}, s32[8,2]{0,1:T(2,128)S(1)}, f32[8,16,128]{2,1,0:T(8,128)S(1)}, s32[]{:T(128)}) %tuple.35), condition=%wide.while_cond.1, body=%wide.while_body.1.sunk | while | flops 2 | bytes 16481 | solution.py:38
  110.9 0.7 bitcast_dynamic-update-slice_fusion.5
  111.7 0.5 slice.35
  112.2 0.7 bitcast_dynamic-update-slice_fusion.5
  112.9 0.5 slice.35
  113.4 0.7 bitcast_dynamic-update-slice_fusion.5
  114.2 0.5 slice.35
  114.7 0.7 bitcast_dynamic-update-slice_fusion.5
  115.5 0.5 slice.35
  116.0 0.7 bitcast_dynamic-update-slice_fusion.5
  116.7 0.5 slice.35
  117.2 0.7 bitcast_dynamic-update-slice_fusion.5
  118.5 0.7 bitcast_dynamic-update-slice_fusion.5
  119.3 0.5 slice.35
  119.8 0.7 bitcast_dynamic-update-slice_fusion.5
  120.5 10.1 %while.2 = (s32[]{:T(128)}, f32[24,128]{1,0:T(8,128)S(1)}, s32[8,2]{0,1:T(2,128)S(1)}, f32[8,16,128]{2,1,0:T(8,128)S(1)}, s32[]{:T(128)}) while((s32[]{:T(128)}, f32[24,128]{1,0:T(8,128)S(1)}, s32[8,2]{0,1:T(2,128)S(1)}, f32[8,16,128]{2,1,0:T(8,128)S(1)}, s32[]{:T(128)}) %tuple.40), condition=%wide.while_cond, body=%wide.while_body.sunk | while | flops 2 | bytes 16481 | solution.py:38
  120.6 0.5 slice.34
  121.1 0.7 bitcast_dynamic-update-slice_fusion.4
  122.4 0.7 bitcast_dynamic-update-slice_fusion.4
  123.1 0.5 slice.34
  123.6 0.7 bitcast_dynamic-update-slice_fusion.4
  124.4 0.5 slice.34
  124.9 0.7 bitcast_dynamic-update-slice_fusion.4
  125.6 0.5 slice.34
  126.1 0.7 bitcast_dynamic-update-slice_fusion.4
  126.9 0.5 slice.34
  127.4 0.7 bitcast_dynamic-update-slice_fusion.4
  128.7 0.7 bitcast_dynamic-update-slice_fusion.4
  129.9 0.7 bitcast_dynamic-update-slice_fusion.4
  130.9 2.5 %multiply_convert_fusion = bf16[8,41,1024]{2,0,1:T(8,128)(2,1)} fusion(f32[8,41,1024]{2,0,1:T(8,128)} %reduce-scatter.2.cloned.1.call-done, f32[8,41]{0,1:T(8,128)S(1)} %copy.45, f32[8,1024]{1,0:T(8,128)S(1)} %get-tuple-element.48, f32[8,41]{0,1:T(8,128)S(1)} %copy.43, f32[8,1024]{1,0:T(8,128)S(1)} %get-tuple-element.47), kind=kLoop, calls=%fused_computation.16 | loop fusion | flops 2015232 | bytes 2083392 | tf_op jit(solution)/shard_map/convert_element_type | solution.py:57
  (71 shorter events, 5.8 us)
Async XLA Ops:
  6.5 4.5 %copy-start.7 = (s32[64]{0:T(128)S(1)}, s32[64]{0:T(128)}, u32[]{:S(2)}) copy-start(s32[64]{0:T(128)} %param.12) | copy-start | bytes 772
  6.5 4.5 %copy-start.6 = (s32[64,8]{0,1:T(8,128)S(1)}, s32[64,8]{0,1:T(8,128)}, u32[]{:S(2)}) copy-start(s32[64,8]{0,1:T(8,128)} %param.10) | copy-start | bytes 6148
  6.5 4.6 %copy-start.3 = (bf16[128,2560]{1,0:T(8,128)(2,1)S(1)}, bf16[128,2560]{1,0:T(8,128)(2,1)}, u32[]{:S(2)}) copy-start(bf16[128,2560]{1,0:T(8,128)(2,1)} %param.9) | copy-start | bytes 1966084
  6.5 5.0 %copy-start.5 = (s32[64,40]{0,1:T(8,128)S(1)}, s32[64,40]{0,1:T(8,128)}, u32[]{:S(2)}) copy-start(s32[64,40]{0,1:T(8,128)} %param.11) | copy-start | bytes 30724
  9.7 68.9 %collective-permute-start = (bf16[1024,1024]{1,0:T(8,128)(2,1)}, bf16[1024,1024]{1,0:T(8,128)(2,1)S(1)}, u32[]{:S(2)}, u32[]{:S(2)}) collective-permute-start(bf16[1024,1024]{1,0:T(8,128)(2,1)} %slice.3), channel_id=1, source_target_pairs={{2,0},{4,2},{6,4},{8,6},{10,8},{12,10},{14,12},{3,1},{5,3},{7,5},{... | collective-permute-start | bytes 6291464 | tf_op jit(solution)/shard_map/ppermute | solution.py:15
  12.4 11.7 %copy-start.8 = (s32[8]{0:T(128)S(1)}, s32[8]{0:T(128)}, u32[]{:S(2)}) copy-start(s32[8]{0:T(128)} %param.13) | copy-start | bytes 100
  15.5 63.0 %all-to-all-start = ((bf16[128,8,320]{0,2,1:T(8,128)(2,1)}), bf16[128,8,320]{0,2,1:T(8,128)(2,1)S(1)}, u32[]{:S(2)}, u32[]{:S(2)}) async-start(bf16[128,8,320]{0,2,1:T(8,128)(2,1)} %bitcast.5), calls=%async_computation | async-start | bytes 1310720 | tf_op jit(solution)/shard_map/all_to_all | solution.py:73
  24.0 106.9 %reduce-scatter.2.cloned.1.call-start = ((), (), s32[]{:S(2)}) async-start(), calls=%async_computation.2 | async-start | bytes 4030464 | tf_op jit(solution)/shard_map/reduce_scatter | solution.py:106
  28.7 51.4 %copy-start.4 = (bf16[8,1024]{1,0:T(8,128)(2,1)S(1)}, bf16[8,1024]{1,0:T(8,128)(2,1)}, u32[]{:S(2)}) copy-start(bf16[8,1024]{1,0:T(8,128)(2,1)} %param.8) | copy-start | bytes 49156
  78.5 1.6 %copy-start.1 = (bf16[128,8,320]{0,2,1:T(8,128)(2,1)}, bf16[128,8,320]{0,2,1:T(8,128)(2,1)S(1)}, u32[]{:S(2)}) copy-start(bf16[128,8,320]{0,2,1:T(8,128)(2,1)S(1)} %all-to-all-done) | copy-start | bytes 1966084
  80.1 4.8 %copy-start = (bf16[3072,1024]{1,0:T(8,128)(2,1)S(1)}, bf16[3072,1024]{1,0:T(8,128)(2,1)}, u32[]{:S(2)}) copy-start(bf16[3072,1024]{1,0:T(8,128)(2,1)} %constant_dynamic-update-slice_fusion) | copy-start | bytes 18874372
  99.8 1.1 copy-start.2
Sparse Core Ops, SparseCore 0:
  99.9 7.5 reduce-scatter.1
where the time goes:
time: 141 us; the launch traced here: 140 us
  waiting for transfers between devices  49.9 us (35%)
  local copies, waits for them, and re-layouts  43.9 us (31%)
  between operations  13.7 us (10%)
  matrix products  10 us (7%)
  starting transfers between devices  9.88 us (7%)
  other arithmetic  9.15 us (6%)
  blocking collectives  3.42 us (2%)
    all_to_all x1, waiting for transfers between devices, shards(): lax.all_to_all(ratios, 'genes', split_axis=1, concat_axis=0, tiled=True)  49.8 us
    gather x48, local copies, waits for them, and re-layouts  19.9 us
    all_to_all x1, starting transfers between devices, shards(): lax.all_to_all(ratios, 'genes', split_axis=1, concat_axis=0, tiled=True)  8.56 us
    unnamed x24, local copies, waits for them, and re-layouts  5.68 us
    reduce_sum x1, other arithmetic, shards(): row_sum = jnp.sum(dose_float, axis=1)  5.48 us
    gather x2, local copies, waits for them, and re-layouts, tile_window(): lax.dynamic_slice_in_dim(tiles, first_tile, width // ALIGN, len(leading))  5.48 us
    dot_general x1, matrix products, shards(): lax.dot_general(expression, dose_rows, (((1,), (1,)), ((), ())), preferre...  4.66 us
    reshape x1, local copies, waits for them, and re-layouts, tile_window(): return piece.reshape(leading + (width,))  3.89 us
  transfers between devices with their start and end apart: 3, of which 1 were waited for; matrix products, arithmetic and copies ran while one was open for 25% of the time, Pallas kernels for 0%

commit v1 on v0

--- a/solution.py
+++ b/solution.py
@@ -70,7 +70,10 @@
     ratios = cluster_ratios(counts, cluster_sizes, valid_mask).reshape(
         intron_counts.shape[0], total_genes * SLOTS
     )
-    exchanged = lax.all_to_all(ratios, "genes", split_axis=1, concat_axis=0, tiled=True)
+    exchanged = jnp.concatenate(
+        lax.all_to_all(jnp.stack(jnp.split(ratios, lax.axis_size("genes"), axis=1)), "genes", 0, 0),
+        axis=0,
+    )
     intron_panel = exchanged.reshape(samp_dev, gene_dev, SLOTS)
     n_samples = lax.axis_size("samples")
     half_width = W // n_samples

time: 141 us -> 141 us (level)
  local copies, waits for them, and re-layouts: 43.9 us -> 49 us
  waiting for transfers between devices: 49.9 us -> 45.5 us
    unnamed x24 -> x31, local copies, waits for them, and re-layouts: 5.68 us -> 10.2 us
    all_to_all x1, waiting for transfers between devices: 49.8 us -> 45.4 us  [shards(): lax.all_to_all(jnp.stack(jnp.split(ratios, lax.axis_size('genes'), axis=1...]
  transfers between devices with their start and end apart: 3 -> 3, of which waited for: 1 -> 1; matrix products, arithmetic and copies ran while one was open for 25% -> 28% of each run, Pallas kernels for 0% -> 0%
where the time goes in v1:
time: 141 us; the launch traced here: 140 us
  local copies, waits for them, and re-layouts  49 us (35%)
  waiting for transfers between devices  45.5 us (32%)
  between operations  13.7 us (10%)
  starting transfers between devices  9.88 us (7%)
  matrix products  9.27 us (7%)
  other arithmetic  9.15 us (6%)
  blocking collectives  3.42 us (2%)
    all_to_all x1, waiting for transfers between devices, shards(): lax.all_to_all(jnp.stack(jnp.split(ratios, lax.axis_size('genes'), axis=1...  45.4 us
    gather x48, local copies, waits for them, and re-layouts  19.9 us
    unnamed x31, local copies, waits for them, and re-layouts  10.2 us
    all_to_all x1, starting transfers between devices, shards(): lax.all_to_all(jnp.stack(jnp.split(ratios, lax.axis_size('genes'), axis=1...  8.56 us
    reduce_sum x1, other arithmetic, shards(): row_sum = jnp.sum(dose_float, axis=1)  5.48 us
    gather x2, local copies, waits for them, and re-layouts, tile_window(): lax.dynamic_slice_in_dim(tiles, first_tile, width // ALIGN, len(leading))  5.48 us
    dot_general x1, matrix products, shards(): lax.dot_general(expression, dose_rows, (((1,), (1,)), ((), ())), preferre...  4.66 us
    reshape x1, local copies, waits for them, and re-layouts, tile_window(): return piece.reshape(leading + (width,))  3.89 us
  transfers between devices with their start and end apart: 3, of which 1 were waited for; matrix products, arithmetic and copies ran while one was open for 28% of the time, Pallas kernels for 0%

profile of v1, /device:TPU:0, one launch (start us, length us, event | category | flops | bytes accessed | tf_op | source)
XLA Modules:
  0.0 140.2 jit_solution(14498258872075226060)
XLA Ops:
  6.5 3.2 %slice.3 = bf16[1024,1024]{1,0:T(8,128)(2,1)} slice(bf16[2048,1024]{1,0:T(8,128)(2,1)} %param.7), slice={[0:1024], [0:1024]} | slice | bytes 4194304 | tf_op jit(solution)/shard_map/slice | solution.py:66
  9.7 1.3 collective-permute-start
  11.7 0.7 gather_fusion
  12.4 2.3 %fusion.3 = bf16[128,64,40]{0,2,1:T(8,128)(2,1)S(1)} fusion(f32[64,40]{1,0:T(8,128)S(1)} %copy.41, bf16[64,128,40]{1,2,0:T(8,128)(2,1)S(1)} %gather_fusion, s32[64,40]{1,0:T(8,128)S(1)} %copy.42, pred[64]{0:T(512)(128)(4,1)S(1)} %compare_and_fusion), kind=kOutput, calls=%fused_computation.15 | convolution fusion | flops 160337920 | bytes 1331264 | tf_op jit(solution)/shard_map/sgj,gjk->sgk/dot_general | solution.py:28
  14.7 0.6 fusion.22
  15.4 0.6 fusion.21
  16.0 0.6 fusion.20
  16.7 0.6 fusion.19
  17.3 0.6 fusion.18
  17.9 0.6 fusion.17
  18.6 0.6 fusion.16
  19.2 0.6 fusion.15
  19.9 8.6 %all-to-all-start = ((bf16[8,128,320]{1,2,0:T(8,128)(2,1)}), bf16[8,128,320]{1,2,0:T(8,128)(2,1)S(1)}, u32[]{:S(2)}, u32[]{:S(2)}) async-start(bf16[8,128,320]{1,2,0:T(8,128)(2,1)} %fusion.15), calls=%async_computation | async-start | bytes 1310720 | tf_op jit(solution)/shard_map/all_to_all | solution.py:74
  28.5 4.6 %constant_dynamic-update-slice_fusion.1 = bf16[3072,1024]{1,0:T(8,128)(2,1)} fusion(bf16[2048,1024]{1,0:T(8,128)(2,1)} %param.7), kind=kLoop, calls=%fused_computation.55 | loop fusion | bytes 8388608
  33.1 45.4 %all-to-all-done = bf16[8,128,320]{1,2,0:T(8,128)(2,1)S(1)} async-done(((bf16[8,128,320]{1,2,0:T(8,128)(2,1)}), bf16[8,128,320]{1,2,0:T(8,128)(2,1)S(1)}, u32[]{:S(2)}, u32[]{:S(2)}) %all-to-all-start) | async-done | bytes 655392 | tf_op jit(solution)/shard_map/all_to_all | solution.py:74
  78.6 1.5 %constant_dynamic-update-slice_fusion = bf16[3072,1024]{1,0:T(8,128)(2,1)} fusion(bf16[3072,1024]{1,0:T(8,128)(2,1)} %constant_dynamic-update-slice_fusion.1, bf16[1024,1024]{1,0:T(8,128)(2,1)S(1)} %collective-permute-done), kind=kLoop, calls=%fused_computation.54 | loop fusion | bytes 4194304 | tf_op jit(solution)/shard_map/concatenate | solution.py:67
  80.1 4.7 %convolution_bitcast_fusion = f32[8,1,24,128]{3,0,2,1:T(8,128)S(1)} fusion(bf16[3072,1024]{1,0:T(8,128)(2,1)} %constant_dynamic-update-slice_fusion, bf16[8,1024]{1,0:T(8,128)(2,1)S(1)} %copy-done.4), kind=kOutput, calls=%fused_computation.22 | convolution fusion | flops 50331648 | bytes 6406144 | tf_op jit(solution)/shard_map/dot_general | solution.py:82
  84.9 2.3 %fusion.26 = f32[8,40,24,128]{3,1,2,0:T(8,128)S(1)} fusion(bf16[8,40,1024,1]{2,1,3,0:T(8,128)(2,1)S(1)} %bitcast.112, bf16[24,128,1024,1]{2,1,0,3:T(8,128)(2,1)S(1)} %bitcast.102), kind=kOutput, calls=%fused_computation.71 | convolution fusion | flops 2013265920 | bytes 10878976 | tf_op jit(solution)/shard_map/dot_general | solution.py:85
  87.2 0.5 pad_maximum_fusion
  87.7 2.7 %copy.46 = f32[8,41,24,128]{3,1,0,2:T(8,128)} copy(f32[8,41,24,128]{3,1,2,0:T(8,128)S(1)} %pad_maximum_fusion) | data formatting | bytes 8060928 | tf_op jit(solution)/shard_map/concatenate | solution.py:89
  90.4 3.1 %gather_fusion.1 = f32[8,41,16,128]{3,1,2,0:T(8,128)S(1)} fusion(f32[8,41,24,128]{3,1,0,2:T(8,128)} %copy.46, s32[8]{0:T(128)S(1)} %or_bitcast_fusion), kind=kCustom, calls=%fused_computation.1 | custom fusion | bytes 5374080 | tf_op jit(solution)/shard_map/vmap()/gather | solution.py:38
  93.5 2.4 %copy.47 = f32[8,41,16,128]{3,2,0,1:T(8,128)} copy(f32[8,41,16,128]{3,1,2,0:T(8,128)S(1)} %gather_fusion.1) | data formatting | bytes 5373952 | tf_op jit(solution)/shard_map/vmap()/gather | solution.py:38
  95.9 3.9 %reshape.51 = f32[8,41,2048]{2,0,1:T(8,128)} reshape(f32[8,41,16,128]{3,2,0,1:T(8,128)} %copy.47) | data formatting | bytes 5373952 | tf_op jit(solution)/shard_map/vmap()/reshape | solution.py:39
  100.2 0.7 copy-done.2
  101.4 5.5 %convert_reduce_fusion = (f32[3072]{0:T(1024)S(1)}, f32[3072]{0:T(1024)S(1)}) fusion(bf16[3072,1024]{1,0:T(8,128)(2,1)} %constant_dynamic-update-slice_fusion), kind=kLoop, calls=%fused_computation.7 | loop fusion | flops 12576768 | bytes 6316032 | tf_op jit(solution)/shard_map/reduce_sum | solution.py:103
  106.9 3.4 %all-reduce.1 = (f32[8,41]{1,0:T(8,128)S(1)}, f32[8,41]{1,0:T(8,128)S(1)}, f32[24,128]{1,0:T(8,128)S(1)}, f32[24,128]{1,0:T(8,128)S(1)}) all-reduce(f32[8,41]{1,0:T(8,128)S(1)} %get-tuple-element.50, f32[8,41]{1,0:T(8,128)S(1)} %get-tuple-element.49, ...), channel_id=1, replica_groups=mesh['parts'=2,'genes'=8,'samples'=2] {'samples'}, use_global_device_ids=true, to_apply=%region_12.13 | all-reduce | flops 6800 | bytes 54400 | tf_op jit(solution)/shard_map/psum | solution.py:105
  110.3 10.1 %while.3 = (s32[]{:T(128)}, f32[24,128]{1,0:T(8,128)S(1)}, s32[8,2]{0,1:T(2,128)S(1)}, f32[8,16,128]{2,1,0:T(8,128)S(1)}, s32[]{:T(128)}) while((s32[]{:T(128)}, f32[24,128]{1,0:T(8,128)S(1)}, s32[8,2]{0,1:T(2,128)S(1)}, f32[8,16,128]{2,1,0:T(8,128)S(1)}, s32[]{:T(128)}) %tuple.35), condition=%wide.while_cond.1, body=%wide.while_body.1.sunk | while | flops 2 | bytes 16481 | solution.py:38
  110.4 0.5 slice.35
  110.9 0.7 bitcast_dynamic-update-slice_fusion.5
  111.7 0.5 slice.35
  112.2 0.7 bitcast_dynamic-update-slice_fusion.5
  112.9 0.5 slice.35
  113.4 0.7 bitcast_dynamic-update-slice_fusion.5
  114.7 0.7 bitcast_dynamic-update-slice_fusion.5
  116.0 0.7 bitcast_dynamic-update-slice_fusion.5
  117.2 0.7 bitcast_dynamic-update-slice_fusion.5
  118.5 0.7 bitcast_dynamic-update-slice_fusion.5
  119.8 0.7 bitcast_dynamic-update-slice_fusion.5
  120.5 10.1 %while.2 = (s32[]{:T(128)}, f32[24,128]{1,0:T(8,128)S(1)}, s32[8,2]{0,1:T(2,128)S(1)}, f32[8,16,128]{2,1,0:T(8,128)S(1)}, s32[]{:T(128)}) while((s32[]{:T(128)}, f32[24,128]{1,0:T(8,128)S(1)}, s32[8,2]{0,1:T(2,128)S(1)}, f32[8,16,128]{2,1,0:T(8,128)S(1)}, s32[]{:T(128)}) %tuple.40), condition=%wide.while_cond, body=%wide.while_body.sunk | while | flops 2 | bytes 16481 | solution.py:38
  121.1 0.7 bitcast_dynamic-update-slice_fusion.4
  122.3 0.7 bitcast_dynamic-update-slice_fusion.4
  123.6 0.7 bitcast_dynamic-update-slice_fusion.4
  124.9 0.7 bitcast_dynamic-update-slice_fusion.4
  126.1 0.7 bitcast_dynamic-update-slice_fusion.4
  127.4 0.7 bitcast_dynamic-update-slice_fusion.4
  128.7 0.7 bitcast_dynamic-update-slice_fusion.4
  129.9 0.7 bitcast_dynamic-update-slice_fusion.4
  130.9 2.5 %multiply_convert_fusion = bf16[8,41,1024]{2,0,1:T(8,128)(2,1)} fusion(f32[8,41,1024]{2,0,1:T(8,128)} %reduce-scatter.2.cloned.1.call-done, f32[8,41]{0,1:T(8,128)S(1)} %copy.51, f32[8,1024]{1,0:T(8,128)S(1)} %get-tuple-element.48, f32[8,41]{0,1:T(8,128)S(1)} %copy.49, f32[8,1024]{1,0:T(8,128)S(1)} %get-tuple-element.47), kind=kLoop, calls=%fused_computation.16 | loop fusion | flops 2015232 | bytes 2083392 | tf_op jit(solution)/shard_map/convert_element_type | solution.py:57
  (79 shorter events, 9.9 us)
Async XLA Ops:
  6.5 4.5 %copy-start.7 = (s32[64]{0:T(128)S(1)}, s32[64]{0:T(128)}, u32[]{:S(2)}) copy-start(s32[64]{0:T(128)} %param.12) | copy-start | bytes 772
  6.5 4.5 %copy-start.3 = (bf16[128,2560]{1,0:T(8,128)(2,1)S(1)}, bf16[128,2560]{1,0:T(8,128)(2,1)}, u32[]{:S(2)}) copy-start(bf16[128,2560]{1,0:T(8,128)(2,1)} %param.9) | copy-start | bytes 1966084
  6.5 4.9 %copy-start.6 = (s32[64,8]{0,1:T(8,128)S(1)}, s32[64,8]{0,1:T(8,128)}, u32[]{:S(2)}) copy-start(s32[64,8]{0,1:T(8,128)} %param.10) | copy-start | bytes 6148
  6.5 5.0 %copy-start.5 = (s32[64,40]{0,1:T(8,128)S(1)}, s32[64,40]{0,1:T(8,128)}, u32[]{:S(2)}) copy-start(s32[64,40]{0,1:T(8,128)} %param.11) | copy-start | bytes 30724
  9.7 68.9 %collective-permute-start = (bf16[1024,1024]{1,0:T(8,128)(2,1)}, bf16[1024,1024]{1,0:T(8,128)(2,1)S(1)}, u32[]{:S(2)}, u32[]{:S(2)}) collective-permute-start(bf16[1024,1024]{1,0:T(8,128)(2,1)} %slice.3), channel_id=1, source_target_pairs={{2,0},{4,2},{6,4},{8,6},{10,8},{12,10},{14,12},{3,1},{5,3},{7,5},{... | collective-permute-start | bytes 6291464 | tf_op jit(solution)/shard_map/ppermute | solution.py:15
  12.4 16.1 %copy-start.8 = (s32[8]{0:T(128)S(1)}, s32[8]{0:T(128)}, u32[]{:S(2)}) copy-start(s32[8]{0:T(128)} %param.13) | copy-start | bytes 100
  19.9 58.6 %all-to-all-start = ((bf16[8,128,320]{1,2,0:T(8,128)(2,1)}), bf16[8,128,320]{1,2,0:T(8,128)(2,1)S(1)}, u32[]{:S(2)}, u32[]{:S(2)}) async-start(bf16[8,128,320]{1,2,0:T(8,128)(2,1)} %fusion.15), calls=%async_computation | async-start | bytes 1310720 | tf_op jit(solution)/shard_map/all_to_all | solution.py:74
  28.4 102.5 %reduce-scatter.2.cloned.1.call-start = ((), (), s32[]{:S(2)}) async-start(), calls=%async_computation.2 | async-start | bytes 4030464 | tf_op jit(solution)/shard_map/reduce_scatter | solution.py:109
  33.0 47.0 %copy-start.4 = (bf16[8,1024]{1,0:T(8,128)(2,1)S(1)}, bf16[8,1024]{1,0:T(8,128)(2,1)}, u32[]{:S(2)}) copy-start(bf16[8,1024]{1,0:T(8,128)(2,1)} %param.8) | copy-start | bytes 49156
  78.5 1.6 %copy-start.1 = (bf16[8,128,320]{1,2,0:T(8,128)(2,1)}, bf16[8,128,320]{1,2,0:T(8,128)(2,1)S(1)}, u32[]{:S(2)}) copy-start(bf16[8,128,320]{1,2,0:T(8,128)(2,1)S(1)} %all-to-all-done) | copy-start | bytes 1966084
  80.1 4.8 %copy-start = (bf16[3072,1024]{1,0:T(8,128)(2,1)S(1)}, bf16[3072,1024]{1,0:T(8,128)(2,1)}, u32[]{:S(2)}) copy-start(bf16[3072,1024]{1,0:T(8,128)(2,1)} %constant_dynamic-update-slice_fusion) | copy-start | bytes 18874372
  99.8 1.1 copy-start.2
Sparse Core Ops, SparseCore 0:
  99.9 7.5 reduce-scatter.1
